TPU v7x, 32 devices: a whole 2x2x4 slice. The times are simulated.
32 devices in a mesh: dp: 8 (over z, x), expert: 4 (over y, core).
Axes of the slice: x: 2, y: 2, z: 4, core: 2. Of those that a mesh axis runs over, the one named last changes fastest.
Arguments:
- tokens: bfloat16 [4096, 2048], P(('dp', 'expert')), may hold values from -6 to 6
- cotangent: bfloat16 [4096, 2048], P(('dp', 'expert')), may hold values from -6 to 6
- expert_ids: int32 [4096, 2], P(('dp', 'expert')), may hold values from 0 to 3, all different within a row; in each aligned block of 128 rows (0 to 127, 128 to 255, ...) at most 72 rows name the same one
- route_share: float32 [4096], P(('dp', 'expert')), may hold values from 0.5 to 0.95
- gate_proj: bfloat16 [4, 7168, 2048], P('expert', 'dp'), may hold values from -0.125 to 0.125
- up_proj: bfloat16 [4, 7168, 2048], P('expert', 'dp'), may hold values from -0.125 to 0.125
- down_anchor: float32 [4, 7168, 2048], P('expert', 'dp'), may hold values from -0.12 to 0.12
- down_average: float32 [4, 7168, 2048], P('expert', 'dp'), may hold values from -0.12 to 0.12
- down_moment: float32 [4, 7168, 2048], P('expert', 'dp'), may hold values from 0.002 to 0.05
Outputs:
- new_anchor: float32 [4, 7168, 2048], P('expert', 'dp')
- new_average: float32 [4, 7168, 2048], P('expert', 'dp')
- new_moment: float32 [4, 7168, 2048], P('expert', 'dp')
Inputs may be any that keep to these rules, and one draw needn't show every extreme that they name: `expert_ids`: the two ids of a token differ. The rows of one device name any expert at most 72 times, and in every draw some device names some expert exactly 72 times.
All inputs are finite; a program needn't handle non-finite values.
Results may differ from a plain program's by a relative error of at most 0.0043.
Values may be sent and summed in bfloat16 or wider, within the bound.
A program may use at most 192 MiB of HBM per device.

v0:
```python
import jax
import jax.numpy as jnp
from jax import lax
from jax.sharding import PartitionSpec as P

FF = 7168
TOPK = 2
beta_one = 0.9
beta_two = 0.95
learn_rate = 0.05
decay_rate = 0.1
step_count = 4.0
epsilon = 1e-08


def expert_terms(pieces, weight_gate, weight_up):
    rows_in, gated_rows = pieces
    gate_act = lax.dot_general(
        rows_in, weight_gate, (((1,), (1,)), ((), ())), preferred_element_type=jnp.float32
    )
    up_act = lax.dot_general(
        rows_in, weight_up, (((1,), (1,)), ((), ())), preferred_element_type=jnp.float32
    )
    hidden = (jax.nn.silu(gate_act) * up_act).astype(jnp.bfloat16)
    return lax.dot_general(
        hidden, gated_rows, (((0,), (0,)), ((), ())), preferred_element_type=jnp.float32
    )


def routed_shards(
    tokens,
    cotangent,
    expert_ids,
    route_share,
    gate_proj,
    up_proj,
    down_anchor,
    down_average,
    down_moment,
):
    experts_all = lax.axis_size("expert")
    tok_rows = tokens.shape[0]
    width = tokens.shape[1]
    capacity = tok_rows * TOPK // experts_all * 9 // 8
    slots = experts_all * capacity
    shares = jnp.stack([route_share, 1.0 - route_share], axis=1)
    expert_range = jnp.arange(experts_all, dtype=jnp.int32)
    flat_ids = expert_ids.reshape(-1)
    onehot_routes = (flat_ids[:, None] == expert_range[None, :]).astype(jnp.int32)
    earlier = jnp.cumsum(onehot_routes, axis=0) - onehot_routes
    slot_of = jnp.sum(earlier * onehot_routes, axis=1)
    target = (flat_ids * capacity + slot_of).reshape(tok_rows, TOPK)
    slot_range = jnp.arange(slots, dtype=jnp.int32)
    placed = target[None, :, :] == slot_range[:, None, None]
    picker = jnp.sum(placed.astype(jnp.float32), axis=2).astype(jnp.bfloat16)
    slot_share = jnp.sum(jnp.where(placed, shares[None, :, :], 0.0), axis=(1, 2))
    send_rows = jnp.dot(picker, tokens, preferred_element_type=jnp.float32).astype(jnp.bfloat16)
    send_grad = (
        slot_share[:, None] * jnp.dot(picker, cotangent, preferred_element_type=jnp.float32)
    ).astype(jnp.bfloat16)
    weight_gate = gate_proj[0]
    weight_up = up_proj[0]
    arrived = (
        lax.all_to_all(
            send_rows.reshape(experts_all, capacity, width),
            "expert",
            split_axis=0,
            concat_axis=0,
            tiled=True,
        ),
        lax.all_to_all(
            send_grad.reshape(experts_all, capacity, width),
            "expert",
            split_axis=0,
            concat_axis=0,
            tiled=True,
        ),
    )
    rows_here = arrived[0].reshape(slots, width)
    grad_here = arrived[1].reshape(slots, width)
    gradient = expert_terms(
        (
            lax.all_gather(rows_here, "dp", axis=0, tiled=True),
            lax.all_gather(grad_here, "dp", axis=0, tiled=True),
        ),
        weight_gate,
        weight_up,
    )
    gradient = gradient[None] * FF ** (-0.5)
    bias_two = 1.0 - beta_two**step_count
    eval_point = (1.0 - beta_one) * down_anchor + beta_one * down_average
    second_moment = beta_two * down_moment + (1.0 - beta_two) * gradient * gradient
    update_dir = gradient / (jnp.sqrt(second_moment / bias_two) + epsilon) + decay_rate * eval_point
    new_anchor = down_anchor - learn_rate * update_dir
    new_average = (1.0 - 1.0 / step_count) * down_average + 1.0 / step_count * new_anchor
    return (new_anchor, new_average, second_moment)


def adam(gradient, down_anchor, down_average, down_moment):
    bias_two = 1.0 - beta_two**step_count
    eval_point = (1.0 - beta_one) * down_anchor + beta_one * down_average
    second_moment = beta_two * down_moment + (1.0 - beta_two) * gradient * gradient
    update_dir = gradient / (jnp.sqrt(second_moment / bias_two) + epsilon) + decay_rate * eval_point
    new_anchor = down_anchor - learn_rate * update_dir
    new_average = (1.0 - 1.0 / step_count) * down_average + 1.0 / step_count * new_anchor
    return (new_anchor, new_average, second_moment)


def expert_shares(expert_ids, route_share, experts):
    shares = jnp.stack([route_share, 1.0 - route_share], axis=0)
    expert_range = jnp.arange(experts, dtype=jnp.int32)
    named = expert_ids.T[:, None, :] == expert_range[None, :, None]
    return jnp.sum(jnp.where(named, shares[:, None, :], 0.0), axis=0)


def dense_shards(
    tokens,
    cotangent,
    expert_ids,
    route_share,
    gate_proj,
    up_proj,
    down_anchor,
    down_average,
    down_moment,
):
    experts_all = lax.axis_size("expert")
    axes = ("dp", "expert")
    table = expert_shares(expert_ids, route_share, experts_all)
    share = lax.all_gather(table, axes, axis=1, tiled=True)
    share = lax.dynamic_index_in_dim(share, lax.axis_index("expert"), 0, keepdims=True)
    rows = lax.all_gather(tokens, axes, axis=0, tiled=True)
    grads = lax.all_gather(cotangent, axes, axis=0, tiled=True)
    dims = (((1,), (1,)), ((), ()))
    gate_act = lax.dot_general(gate_proj[0], rows, dims, preferred_element_type=jnp.float32)
    up_act = lax.dot_general(up_proj[0], rows, dims, preferred_element_type=jnp.float32)
    hidden = (jax.nn.silu(gate_act) * up_act * share).astype(jnp.bfloat16)
    gradient = jnp.dot(hidden, grads, preferred_element_type=jnp.float32)
    return adam(gradient[None] * FF ** (-0.5), down_anchor, down_average, down_moment)


def solution(mesh):
    placed = (
        P(("dp", "expert"), None),
        P(("dp", "expert"), None),
        P(("dp", "expert"), None),
        P(("dp", "expert")),
        P("expert", "dp", None),
        P("expert", "dp", None),
        P("expert", "dp", None),
        P("expert", "dp", None),
        P("expert", "dp", None),
    )
    shards = dense_shards if mesh.shape["expert"] <= 2 * TOPK else routed_shards
    return jax.shard_map(
        shards,
        mesh=mesh,
        in_specs=placed,
        out_specs=(P("expert", "dp", None), P("expert", "dp", None), P("expert", "dp", None)),
        check_vma=False,
    )
```

profile of v0, /device:TPU:0, one launch (start us, length us, event | category | flops | bytes accessed | tf_op | source)
XLA Modules:
  0.0 284.1 jit_solution(15623975847709586878)
XLA Ops:
  7.2 0.0 all-gather.3.cloned.1.call-start
  7.2 0.7 all-gather.3.cloned.1.call-update
  7.9 0.0 all-gather.5.cloned.1.call-start
  7.9 0.7 all-gather.5.cloned.1.call-update
  8.7 0.7 subtract_bitcast_fusion
  9.3 0.7 pad_maximum_fusion
  10.0 0.7 select_reduce_fusion
  10.7 44.2 %all_gather.10 = f32[4,4096]{1,0:T(4,128)S(1)} all-gather(f32[4,128]{1,0:T(4,128)S(1)} %select_reduce_fusion), channel_id=1, replica_groups=mesh['dp'=8,'expert'=4] {'dp','expert'}, dimensions={1}, use_global_device_ids=true | all-gather | bytes 67584 | tf_op jit(solution)/shard_map/all_gather | solution.py:130
  54.9 73.1 %all-gather.3.cloned.1.call-done = bf16[4096,2048]{1,0:T(8,128)(2,1)} async-done(((bf16[128,2048]{1,0:T(8,128)(2,1)}), bf16[4096,2048]{1,0:T(8,128)(2,1)}) %all-gather.3.cloned.1.call-update) | async-done | bytes 16777232 | tf_op jit(solution)/shard_map/all_gather | solution.py:132
  128.0 0.0 copy-start
  128.0 21.3 %fusion.4 = f32[896,4096]{1,0:T(8,128)} fusion(bf16[4096,2048]{1,0:T(8,128)(2,1)} %all-gather.3.cloned.1.call-done, bf16[1,896,2048]{2,1,0:T(8,128)(2,1)} %param.13), kind=kOutput, calls=%fused_computation.8 | convolution fusion | flops 15032385536 | bytes 35127296 | tf_op jit(solution)/shard_map/dot_general | solution.py:135
  149.3 0.0 copy-done
  149.3 23.7 %multiply_convert_fusion = bf16[896,4096]{1,0:T(8,128)(2,1)} fusion(f32[896,4096]{1,0:T(8,128)} %fusion.4, bf16[4096,2048]{1,0:T(8,128)(2,1)} %all-gather.3.cloned.1.call-done, f32[4096]{0:T(1024)S(1)} %bitcast.27, bf16[1,896,2048]{2,1,0:T(8,128)(2,1)S(1)} %copy-done), kind=kOutput, calls=%fused_computation | convolution fusion | flops 15058075648 | bytes 42483712 | tf_op jit(solution)/shard_map/dot_general | solution.py:136
  173.0 70.5 %all-gather.5.cloned.1.call-done = bf16[4096,2048]{1,0:T(8,128)(2,1)} async-done(((bf16[128,2048]{1,0:T(8,128)(2,1)}), bf16[4096,2048]{1,0:T(8,128)(2,1)}) %all-gather.5.cloned.1.call-update) | async-done | bytes 16777232 | tf_op jit(solution)/shard_map/all_gather | solution.py:133
  243.5 33.8 %multiply_add_fusion = (f32[1,896,2048]{2,1,0:T(8,128)}, f32[1,896,2048]{2,1,0:T(8,128)}, f32[1,896,2048]{2,1,0:T(8,128)}) fusion(f32[1,896,2048]{2,1,0:T(8,128)} %param.16, f32[1,896,2048]{2,1,0:T(8,128)} %param.15, f32[1,896,2048]{2,1,0:T(8,128)} %param.17, bf16[896,4096]{1,0:T(8,128)(2,1)} %multiply_convert_fusion, ...), kind=kOutput, calls=%fused_computation.6 | convolution fusion | flops 15065415680 | bytes 68157440 | tf_op jit(solution)/shard_map/dot_general | solution.py:138
  (1 shorter events, 0.0 us)
Async XLA Ops:
  7.2 120.8 %all-gather.3.cloned.1.call-start = ((), (), s32[]{:S(2)}) async-start(), calls=%async_computation | async-start | bytes 17301504 | tf_op jit(solution)/shard_map/all_gather | solution.py:132
  7.9 235.6 %all-gather.5.cloned.1.call-start = ((), (), s32[]{:S(2)}) async-start(), calls=%async_computation.1 | async-start | bytes 17301504 | tf_op jit(solution)/shard_map/all_gather | solution.py:133
  128.0 21.3 %copy-start = (bf16[1,896,2048]{2,1,0:T(8,128)(2,1)S(1)}, bf16[1,896,2048]{2,1,0:T(8,128)(2,1)}, u32[]{:S(2)}) copy-start(bf16[1,896,2048]{2,1,0:T(8,128)(2,1)} %param.14) | copy-start | bytes 11010052
Sparse Core Ops, SparseCore 0:
  10.8 117.1 all-gather.2
  130.9 112.5 all-gather.4
where the time goes:
time: 284 us
  waiting for transfers between devices  145 us (51%)
  matrix products  78.8 us (28%)
  blocking collectives  44.2 us (16%)
  between operations  14 us (5%)
    all_gather x1, waiting for transfers between devices, dense_shards(): rows = lax.all_gather(tokens, axes, axis=0, tiled=True)  73.1 us
    all_gather x1, waiting for transfers between devices, dense_shards(): grads = lax.all_gather(cotangent, axes, axis=0, tiled=True)  70.5 us
    all_gather x1, blocking collectives, dense_shards(): share = lax.all_gather(table, axes, axis=1, tiled=True)  44.2 us
    dot_general x1, matrix products, dense_shards(): gradient = jnp.dot(hidden, grads, preferred_element_type=jnp.float32)  33.8 us
    dot_general x1, matrix products, dense_shards(): lax.dot_general(up_proj[0], rows, dims, preferred_element_type=jnp.float32)  23.7 us
    dot_general x1, matrix products, dense_shards(): lax.dot_general(gate_proj[0], rows, dims, preferred_element_type=jnp.floa...  21.3 us
  transfers between devices with their start and end apart: 2, of which 2 were waited for; matrix products, arithmetic and copies ran while one was open for 17% of the time, Pallas kernels for 0%

commit v1 on v0

--- a/solution.py
+++ b/solution.py
@@ -127,7 +127,7 @@
     experts_all = lax.axis_size("expert")
     axes = ("dp", "expert")
     table = expert_shares(expert_ids, route_share, experts_all)
-    share = lax.all_gather(table, axes, axis=1, tiled=True)
+    share = jnp.concatenate(lax.all_gather(table, axis_name=axes), axis=1)
     share = lax.dynamic_index_in_dim(share, lax.axis_index("expert"), 0, keepdims=True)
     rows = lax.all_gather(tokens, axes, axis=0, tiled=True)
     grads = lax.all_gather(cotangent, axes, axis=0, tiled=True)

time: 284 us -> 284 us (level)
  no operation moved by 1% of the time
where the time goes in v1:
time: 284 us
  waiting for transfers between devices  145 us (51%)
  matrix products  78.8 us (28%)
  blocking collectives  44.2 us (16%)
  between operations  14 us (5%)
    all_gather x1, waiting for transfers between devices, dense_shards(): rows = lax.all_gather(tokens, axes, axis=0, tiled=True)  73.1 us
    all_gather x1, waiting for transfers between devices, dense_shards(): grads = lax.all_gather(cotangent, axes, axis=0, tiled=True)  70.5 us
    all_gather x1, blocking collectives, dense_shards(): share = jnp.concatenate(lax.all_gather(table, axis_name=axes), axis=1)  44.2 us
    dot_general x1, matrix products, dense_shards(): gradient = jnp.dot(hidden, grads, preferred_element_type=jnp.float32)  33.8 us
    dot_general x1, matrix products, dense_shards(): lax.dot_general(up_proj[0], rows, dims, preferred_element_type=jnp.float32)  23.7 us
    dot_general x1, matrix products, dense_shards(): lax.dot_general(gate_proj[0], rows, dims, preferred_element_type=jnp.floa...  21.3 us
  transfers between devices with their start and end apart: 2, of which 2 were waited for; matrix products, arithmetic and copies ran while one was open for 17% of the time, Pallas kernels for 0%

profile of v1, /device:TPU:0, one launch (start us, length us, event | category | flops | bytes accessed | tf_op | source)
XLA Modules:
  0.0 284.1 jit_solution(7384932164250804194)
XLA Ops:
  7.2 0.0 all-gather.5.cloned.1.call-start
  7.2 0.7 all-gather.5.cloned.1.call-update
  7.9 0.0 all-gather.7.cloned.1.call-start
  7.9 0.7 all-gather.7.cloned.1.call-update
  8.7 0.7 subtract_bitcast_fusion
  9.3 0.7 pad_maximum_fusion
  10.0 0.7 select_reduce_fusion
  10.7 44.2 %all-gather.1 = f32[32,4,128]{2,1,0:T(4,128)S(1)} all-gather(f32[1,4,128]{2,1,0:T(4,128)S(1)} %bitcast.33), channel_id=2, replica_groups=mesh['dp'=8,'expert'=4] {'dp','expert'}, dimensions={0}, use_global_device_ids=true | all-gather | bytes 67584 | tf_op jit(solution)/shard_map/all_gather | solution.py:130
  54.9 73.1 %all-gather.5.cloned.1.call-done = bf16[4096,2048]{1,0:T(8,128)(2,1)} async-done(((bf16[128,2048]{1,0:T(8,128)(2,1)}), bf16[4096,2048]{1,0:T(8,128)(2,1)}) %all-gather.5.cloned.1.call-update) | async-done | bytes 16777232 | tf_op jit(solution)/shard_map/all_gather | solution.py:132
  128.0 0.0 copy-start
  128.0 21.3 %fusion.4 = f32[896,4096]{1,0:T(8,128)} fusion(bf16[4096,2048]{1,0:T(8,128)(2,1)} %all-gather.5.cloned.1.call-done, bf16[1,896,2048]{2,1,0:T(8,128)(2,1)} %param.13), kind=kOutput, calls=%fused_computation.8 | convolution fusion | flops 15032385536 | bytes 35127296 | tf_op jit(solution)/shard_map/dot_general | solution.py:135
  149.3 0.0 copy-done
  149.3 23.7 %multiply_convert_fusion = bf16[896,4096]{1,0:T(8,128)(2,1)} fusion(f32[896,4096]{1,0:T(8,128)} %fusion.4, bf16[4096,2048]{1,0:T(8,128)(2,1)} %all-gather.5.cloned.1.call-done, f32[4096]{0:T(1024)S(1)} %bitcast.32, bf16[1,896,2048]{2,1,0:T(8,128)(2,1)S(1)} %copy-done), kind=kOutput, calls=%fused_computation | convolution fusion | flops 15058075648 | bytes 42483712 | tf_op jit(solution)/shard_map/dot_general | solution.py:136
  173.0 70.5 %all-gather.7.cloned.1.call-done = bf16[4096,2048]{1,0:T(8,128)(2,1)} async-done(((bf16[128,2048]{1,0:T(8,128)(2,1)}), bf16[4096,2048]{1,0:T(8,128)(2,1)}) %all-gather.7.cloned.1.call-update) | async-done | bytes 16777232 | tf_op jit(solution)/shard_map/all_gather | solution.py:133
  243.5 33.8 %multiply_add_fusion = (f32[1,896,2048]{2,1,0:T(8,128)}, f32[1,896,2048]{2,1,0:T(8,128)}, f32[1,896,2048]{2,1,0:T(8,128)}) fusion(f32[1,896,2048]{2,1,0:T(8,128)} %param.16, f32[1,896,2048]{2,1,0:T(8,128)} %param.15, f32[1,896,2048]{2,1,0:T(8,128)} %param.17, bf16[896,4096]{1,0:T(8,128)(2,1)} %multiply_convert_fusion, ...), kind=kOutput, calls=%fused_computation.6 | convolution fusion | flops 15065415680 | bytes 68157440 | tf_op jit(solution)/shard_map/dot_general | solution.py:138
  (1 shorter events, 0.0 us)
Async XLA Ops:
  7.2 120.8 %all-gather.5.cloned.1.call-start = ((), (), s32[]{:S(2)}) async-start(), calls=%async_computation | async-start | bytes 17301504 | tf_op jit(solution)/shard_map/all_gather | solution.py:132
  7.9 235.6 %all-gather.7.cloned.1.call-start = ((), (), s32[]{:S(2)}) async-start(), calls=%async_computation.1 | async-start | bytes 17301504 | tf_op jit(solution)/shard_map/all_gather | solution.py:133
  128.0 21.3 %copy-start = (bf16[1,896,2048]{2,1,0:T(8,128)(2,1)S(1)}, bf16[1,896,2048]{2,1,0:T(8,128)(2,1)}, u32[]{:S(2)}) copy-start(bf16[1,896,2048]{2,1,0:T(8,128)(2,1)} %param.14) | copy-start | bytes 11010052
Sparse Core Ops, SparseCore 0:
  10.8 117.1 all-gather.4
  130.9 112.5 all-gather.6

commit v2 on v0

--- a/solution.py
+++ b/solution.py
@@ -129,8 +129,13 @@
     table = expert_shares(expert_ids, route_share, experts_all)
     share = lax.all_gather(table, axes, axis=1, tiled=True)
     share = lax.dynamic_index_in_dim(share, lax.axis_index("expert"), 0, keepdims=True)
-    rows = lax.all_gather(tokens, axes, axis=0, tiled=True)
-    grads = lax.all_gather(cotangent, axes, axis=0, tiled=True)
+    rows, grads = jnp.split(
+        lax.all_gather(
+            jnp.concatenate([tokens, cotangent], axis=1), axis_name=axes, axis=0, tiled=True
+        ),
+        [tokens.shape[1]],
+        axis=1,
+    )
     dims = (((1,), (1,)), ((), ()))
     gate_act = lax.dot_general(gate_proj[0], rows, dims, preferred_element_type=jnp.float32)
     up_act = lax.dot_general(up_proj[0], rows, dims, preferred_element_type=jnp.float32)

time: 284 us -> 296 us (1.042)
  waiting for transfers between devices: 145 us -> 153 us
    all_gather x2 -> x1, waiting for transfers between devices: 144 us -> 153 us  [dense_shards(): lax.all_gather(jnp.concatenate([tokens, cotangent], axis=1), axis_name=ax...]
  transfers between devices with their start and end apart: 2 -> 1, of which waited for: 2 -> 1; matrix products, arithmetic and copies ran while one was open for 17% -> 1% of each run, Pallas kernels for 0% -> 0%
where the time goes in v2:
time: 296 us
  waiting for transfers between devices  153 us (52%)
  matrix products  80.2 us (27%)
  blocking collectives  44.3 us (15%)
  between operations  14 us (5%)
  other arithmetic  4.28 us (1%)
    all_gather x1, waiting for transfers between devices, dense_shards(): lax.all_gather(jnp.concatenate([tokens, cotangent], axis=1), axis_name=ax...  153 us
    all_gather x1, blocking collectives, dense_shards(): share = lax.all_gather(table, axes, axis=1, tiled=True)  44.3 us
    dot_general x1, matrix products, dense_shards(): gradient = jnp.dot(hidden, grads, preferred_element_type=jnp.float32)  31.1 us
    dot_general x1, matrix products, dense_shards(): lax.dot_general(up_proj[0], rows, dims, preferred_element_type=jnp.float32)  25.6 us
    dot_general x1, matrix products, dense_shards(): lax.dot_general(gate_proj[0], rows, dims, preferred_element_type=jnp.floa...  23.5 us
  transfers between devices with their start and end apart: 1, of which 1 were waited for; matrix products, arithmetic and copies ran while one was open for 1% of the time, Pallas kernels for 0%

profile of v2, /device:TPU:0, one launch (start us, length us, event | category | flops | bytes accessed | tf_op | source)
XLA Modules:
  0.0 295.6 jit_solution(12949898858500436917)
XLA Ops:
  7.2 0.0 all-gather.2.cloned.1.call-start
  7.2 2.3 pad_maximum_fusion
  9.5 0.0 all-gather.2.cloned.1.call-update
  9.5 0.7 subtract_bitcast_fusion
  10.2 0.7 pad_maximum_fusion.1
  10.8 0.7 select_reduce_fusion
  11.5 44.3 %all_gather.7 = f32[4,4096]{1,0:T(4,128)S(1)} all-gather(f32[4,128]{1,0:T(4,128)S(1)} %select_reduce_fusion), channel_id=1, replica_groups=mesh['dp'=8,'expert'=4] {'dp','expert'}, dimensions={1}, use_global_device_ids=true | all-gather | bytes 67584 | tf_op jit(solution)/shard_map/all_gather | solution.py:130
  55.8 152.7 %all-gather.2.cloned.1.call-done = bf16[4096,4096]{1,0:T(8,128)(2,1)} async-done(((bf16[128,4096]{1,0:T(8,128)(2,1)}), bf16[4096,4096]{1,0:T(8,128)(2,1)}) %all-gather.2.cloned.1.call-update) | async-done | bytes 33554448 | tf_op jit(solution)/shard_map/all_gather | solution.py:133
  208.5 0.0 copy-start
  208.5 23.5 %fusion.4 = f32[4096,896]{1,0:T(8,128)} fusion(bf16[4096,4096]{1,0:T(8,128)(2,1)} %all-gather.2.cloned.1.call-done, bf16[1,896,2048]{2,1,0:T(8,128)(2,1)} %param.13), kind=kOutput, calls=%fused_computation.4 | convolution fusion | flops 15032385536 | bytes 35127296 | tf_op jit(solution)/shard_map/dot_general | solution.py:140
  232.1 0.0 copy-done
  232.1 25.6 %fusion.7.clone.1.clone.5 = bf16[896,4096]{0,1:T(8,128)(2,1)} fusion(f32[4096,896]{1,0:T(8,128)} %fusion.4, bf16[4096,4096]{1,0:T(8,128)(2,1)} %all-gather.2.cloned.1.call-done, f32[4096]{0:T(1024)S(1)} %bitcast.66, bf16[1,896,2048]{2,1,0:T(8,128)(2,1)S(1)} %copy-done), kind=kOutput, calls=%fused_computation.8.clone.clone.clone.clone.clone.2 | convolution fusion | flops 15058075648 | bytes 42483712 | tf_op jit(solution)/shard_map/dot_general | solution.py:141
  257.7 31.1 %multiply_add_fusion = (f32[1,896,2048]{2,1,0:T(8,128)}, f32[1,896,2048]{2,1,0:T(8,128)}, f32[1,896,2048]{2,1,0:T(8,128)}) fusion(f32[1,896,2048]{2,1,0:T(8,128)} %param.16, f32[1,896,2048]{2,1,0:T(8,128)} %param.15, f32[1,896,2048]{2,1,0:T(8,128)} %param.17, bf16[4096,4096]{1,0:T(8,128)(2,1)} %all-gather.2.cloned.1.call-done, ...), kind=kOutput, calls=%fused_computation.19 | convolution fusion | flops 15065415680 | bytes 68157440 | tf_op jit(solution)/shard_map/dot_general | solution.py:143
  (1 shorter events, 0.0 us)
Async XLA Ops:
  7.2 201.4 %all-gather.2.cloned.1.call-start = ((), (), s32[]{:S(2)}) async-start(), calls=%async_computation | async-start | bytes 34603008 | tf_op jit(solution)/shard_map/all_gather | solution.py:133
  208.5 23.5 %copy-start = (bf16[1,896,2048]{2,1,0:T(8,128)(2,1)S(1)}, bf16[1,896,2048]{2,1,0:T(8,128)(2,1)}, u32[]{:S(2)}) copy-start(bf16[1,896,2048]{2,1,0:T(8,128)(2,1)} %param.14) | copy-start | bytes 11010052
Sparse Core Ops, SparseCore 0:
  11.4 197.0 all-gather.1
